TPU v7x, 32 devices: a whole 2x2x4 slice. The times are simulated.
32 devices in a mesh: feat: 8 (over y, x, core), rep: 4 (over z).
Axes of the slice: x: 2, y: 2, z: 4, core: 2. Of those that a mesh axis runs over, the one named last changes fastest.
Arguments:
- features: bfloat16 [4, 8, 1024, 512], P('rep', None, 'feat'), may hold values from -6 to 6
- adjacency_one: int32 [4, 8, 5, 16, 512], P('rep'), may hold values from 0 to 65535, as said below
- pre_hidden: bfloat16 [4, 8, 256, 256], P('rep', 'feat'), may hold values from -6 to 6
- adjacency_two: int32 [4, 8, 5, 8, 256], P('rep', 'feat'), may hold values from 0 to 65535, as said below
- weight_two: bfloat16 [6, 256, 256], replicated, may hold values from -0.375 to 0.375
- out_grad: bfloat16 [4, 8, 128, 256], P('rep', 'feat'), may hold values from -6 to 6
Outputs:
- grad_w1: float32 [6, 1024, 256], P(None, 'feat')
- grad_b1: float32 [256], replicated
- grad_w2: float32 [6, 256, 256], replicated
- grad_b2: float32 [256], replicated
Inputs may be any that keep to these rules, and one draw needn't show every extreme that they name: `adjacency_one`: bit k, k below 16, of word (w, n) is the entry of destination row 16 w + k and source column n; higher bits are zero; some rows are empty. `adjacency_two`: bit k, k below 16, of word (w, n) is the entry of seed row 16 w + k and source column n; higher bits are zero; some rows are empty.
All inputs are finite; a program needn't handle non-finite values.
Results may differ from a plain program's by a relative error of at most 0.0041.
Values may be sent and summed in bfloat16 or wider, within the bound.
No kernel may reach another device: no remote copies, remote signals or barrier semaphores. Data moves between devices by JAX's collectives and lax.ppermute only.
A program may use at most 128 MiB of HBM per device.

v0:
```python
import math
import jax
import jax.numpy as jnp
from jax import lax
from jax.sharding import PartitionSpec as P


def unpack(packed):
    shifts = jnp.arange(16, dtype=jnp.int32)
    spread = jnp.bitwise_and(jnp.right_shift(packed[..., None, :], shifts[:, None]), 1)
    dense = spread.reshape(packed.shape[:-2] + (packed.shape[-2] * 16, packed.shape[-1]))
    degree = jnp.sum(dense, axis=-1).astype(jnp.float32)
    return (dense.astype(jnp.bfloat16), 1.0 / jnp.maximum(degree, 1.0))


def upper_layer(pre_rows, words_two, grad_rows, weight_two, factor):
    hidden = jnp.maximum(pre_rows, 0)
    seed_count = grad_rows.shape[0]
    matrix, inverse = unpack(words_two)
    mixed = (
        jnp.einsum("rsd,dh->rsh", matrix, hidden, preferred_element_type=jnp.float32)
        * inverse[..., None]
    ).astype(jnp.bfloat16)
    scaled = grad_rows.astype(jnp.float32) * factor
    scaled_low = scaled.astype(jnp.bfloat16)
    grad_rel = jnp.einsum("rsh,sk->rhk", mixed, scaled_low, preferred_element_type=jnp.float32)
    grad_self = jnp.einsum(
        "sh,sk->hk", hidden[:seed_count], scaled_low, preferred_element_type=jnp.float32
    )
    weight_grad = jnp.concatenate([grad_self[None], grad_rel], 0)
    backed = (
        jnp.einsum("sk,rhk->rsh", scaled_low, weight_two[1:], preferred_element_type=jnp.float32)
        * inverse[..., None]
    ).astype(jnp.bfloat16)
    spread_back = jnp.einsum("rsd,rsh->dh", matrix, backed, preferred_element_type=jnp.float32)
    own_part = jnp.einsum(
        "sk,hk->sh", scaled_low, weight_two[0], preferred_element_type=jnp.float32
    )
    hidden_total = spread_back + jnp.pad(own_part, ((0, hidden.shape[0] - seed_count), (0, 0)))
    hidden_grad = jnp.where(pre_rows > 0, hidden_total, 0.0).astype(jnp.bfloat16)
    return (
        weight_grad,
        jnp.sum(scaled, 0),
        hidden_grad,
        jnp.sum(hidden_grad.astype(jnp.float32), 0),
    )


def panel_terms(word_block, column_block, grad_block):
    matrix, inverse = unpack(word_block)
    rows_one = grad_block.shape[1]
    gathered = (
        jnp.einsum("brdn,bcn->brdc", matrix, column_block, preferred_element_type=jnp.float32)
        * inverse[..., None]
    ).astype(jnp.bfloat16)
    panel_rel = jnp.einsum(
        "brdc,bdh->rch", gathered, grad_block, preferred_element_type=jnp.float32
    )
    panel_self = jnp.einsum(
        "bcd,bdh->ch", column_block[:, :, :rows_one], grad_block, preferred_element_type=jnp.float32
    )
    return jnp.concatenate([panel_self[None], panel_rel], 0)


def on_device(features, adjacency_one, pre_hidden, adjacency_two, weight_two, out_grad):
    seed_count = out_grad.shape[2]
    factor = float(seed_count * lax.axis_size("feat") * lax.axis_size("rep")) ** (-0.5)
    weight_grad, bias_two, hidden_grad, bias_one = upper_layer(
        pre_hidden[0, 0], adjacency_two[0, 0], out_grad[0, 0], weight_two, factor
    )
    feature_local = features[0]
    adj_local = adjacency_one[0]
    col_width = feature_local.shape[1]
    hidden_width = hidden_grad.shape[1]
    relations = adj_local.shape[1]
    initial = jnp.zeros((relations + 1, col_width, hidden_width), jnp.float32)
    piece = lax.all_gather(hidden_grad[None], "feat", axis=0, tiled=True)
    piece_rows = piece.shape[0]
    group_size = math.gcd(piece_rows, 8)
    turn_count = piece_rows // group_size
    word_block = adj_local
    word_block = word_block.reshape((turn_count, group_size) + adj_local.shape[1:])
    column_block = feature_local
    column_block = column_block.reshape((turn_count, group_size) + feature_local.shape[1:])
    grad_block = piece.reshape((turn_count, group_size) + piece.shape[1:])

    def one_turn(running, inputs):
        return (running + panel_terms(inputs[0], inputs[1], inputs[2]), None)

    running, unused = lax.scan(one_turn, initial, (word_block, column_block, grad_block))
    grad_w1 = lax.psum(running, "rep")
    grad_w2, grad_b1, grad_b2 = lax.psum((weight_grad, bias_one, bias_two), ("feat", "rep"))
    return (grad_w1, grad_b1, grad_w2, grad_b2)


def solution(mesh):
    placed = (
        P("rep", None, "feat", None),
        P("rep", None, None, None, None),
        P("rep", "feat", None, None),
        P("rep", "feat", None, None, None),
        P(),
        P("rep", "feat", None, None),
    )
    return jax.shard_map(
        on_device,
        mesh=mesh,
        in_specs=placed,
        out_specs=(P(None, "feat", None), P(), P(), P()),
        check_vma=False,
    )
```

profile of v0, /device:TPU:0, one launch (start us, length us, event | category | flops | bytes accessed | tf_op | source)
XLA Modules:
  0.0 213.1 jit_solution(5158156742498113044)
XLA Ops:
  8.0 0.0 copy-start
  8.0 0.0 all-gather.3.cloned.1.call-start
  8.1 1.6 fusion.28
  9.7 0.1 div.22
  9.8 0.1 shift_right_arithmetic.72
  9.9 0.9 fusion.27
  10.8 1.1 fusion.37
  11.9 2.4 %convert_reduce_fusion = (f32[256]{0:T(256)S(1)}, bf16[256,256]{1,0:T(8,128)(2,1)}) fusion(f32[128,256]{1,0:T(8,128)S(1)} %fusion.37, bf16[5,128,256]{2,1,0:T(8,128)(2,1)S(1)} %fusion.27, bf16[6,256,256]{2,1,0:T(8,128)(2,1)} %param.10, f32[5,128]{1,0:T(8,128)S(1)} %div.22, bf16[1,1,128,256]{3,2,1,0:T(8,128)(2,1)} %param.11, bf16[1,1,256,256]{3,2,1,0:T(8,128)(2,1)} %param.8), kind=kOutput, calls=%fused_computation.38 | convolution fusion | flops 168722176 | bytes 1445376 | tf_op jit(solution)/shard_map/rsd,rsh->dh/dot_general | solution.py:35
  14.4 0.0 all-gather.3.cloned.1.call-update
  14.4 0.0 all-reduce.7.cloned.1.call-start
  14.4 0.9 broadcast_maximum_fusion
  15.4 1.0 convolution_bitcast_fusion.1
  16.4 1.6 fusion.19
  18.0 1.2 pad_maximum_fusion
  19.3 0.0 all-reduce.7.cloned.1.call-update
  19.3 0.2 all-reduce.5.cloned.1.call-start
  19.5 0.0 copy-done
  19.5 10.9 %and_reduce_fusion = s32[8,5,16,16]{3,2,1,0:T(8,128)S(1)} fusion(s32[8,5,16,512]{3,2,1,0:T(8,128)S(1)} %bitcast.90), kind=kLoop, calls=%fused_computation.3 | loop fusion | flops 15718400 | bytes 1351680 | tf_op jit(solution)/shard_map/while/body/eval_jaxpr/reduce_sum | solution.py:12
  30.4 0.1 maximum_divide_fusion
  30.5 0.2 reshape.90
  30.7 0.1 shift_right_arithmetic.81
  30.7 10.1 %all-gather.3.cloned.1.call-done = bf16[2048,256]{1,0:T(8,128)(2,1)} async-done(((bf16[256,256]{1,0:T(8,128)(2,1)}), bf16[2048,256]{1,0:T(8,128)(2,1)}) %all-gather.3.cloned.1.call-update) | async-done | bytes 1048592 | tf_op jit(solution)/shard_map/all_gather | solution.py:77
  40.9 0.0 copy-start.2
  40.9 0.0 copy-start.3
  40.9 10.5 %shift_right_arithmetic.78 = s32[8,5,16,16,512]{4,3,2,1,0:T(8,128)} broadcast(s32[8,5,16,512]{3,2,1,0:T(8,128)S(1)} %bitcast.91), dimensions={0,1,2,4} | broadcast | bytes 22282240 | tf_op jit(solution)/shard_map/while/body/eval_jaxpr/shift_right_arithmetic | solution.py:10
  51.3 0.0 copy-done.2
  51.3 0.0 copy-done.3
  51.3 0.0 copy-start.1
  51.3 9.5 %fusion.13 = f32[5,128,256]{2,1,0:T(8,128)S(1)} fusion(bf16[8,256,256,1]{2,1,0,3:T(8,128)(2,1)S(1)} %bitcast.96, f32[8,5,256]{2,0,1:T(8,128)S(1)} %copy.37, s32[8,5,256,512]{3,2,1,0:T(8,128)} %bitcast.89, s32[256]{0:T(256)S(1)} %shift_right_arithmetic.81, bf16[1,8,128,512]{3,2,1,0:T(8,128)(2,1)S(1)} %copy-done.2), kind=kOutput, calls=%fused_computation.14 | convolution fusion | flops 2031616000 | bytes 23766016 | tf_op jit(solution)/shard_map/while/body/eval_jaxpr/brdc,bdh->rch/dot_general | solution.py:56
  60.8 0.5 convolution_bitcast_fusion.2
  61.3 0.1 copy.30
  61.4 1.0 pad_maximum_fusion.1
  62.4 0.0 all-reduce.5.cloned.1.call-update
  62.4 0.0 copy-done.1
  62.4 39.3 %all-reduce.1 = (f32[256]{0:T(256)}, f32[256]{0:T(256)}) all-reduce(f32[256]{0:T(256)S(1)} %get-tuple-element.23, f32[256]{0:T(256)S(1)} %fusion.40), channel_id=1, replica_groups=mesh['feat'=8,'rep'=4] {'feat','rep'}, use_global_device_ids=true, to_apply=%region_4.5 | all-reduce | flops 512 | bytes 4096 | tf_op jit(solution)/shard_map/psum | solution.py:92
  101.8 53.7 %all-reduce.7.cloned.1.call-done = f32[6,256,256]{2,1,0:T(8,128)} async-done(((f32[6,256,256]{2,1,0:T(8,128)}), f32[6,256,256]{2,1,0:T(8,128)}) %all-reduce.7.cloned.1.call-update) | async-done | bytes 1572880 | tf_op jit(solution)/shard_map/psum | solution.py:92
  155.4 45.4 %all-reduce.5.cloned.1.call-done = f32[6,128,256]{2,1,0:T(8,128)} async-done(((f32[6,128,256]{2,1,0:T(8,128)}), f32[6,128,256]{2,1,0:T(8,128)}) %all-reduce.5.cloned.1.call-update) | async-done | bytes 786448 | tf_op jit(solution)/shard_map/psum | solution.py:91
  200.8 2.1 copy.52
  202.9 2.7 %copy.53 = f32[6,256,256]{2,1,0:T(8,128)} copy(f32[6,256,256]{2,1,0:T(8,128)} %all-reduce.7.cloned.1.call-done) | data formatting | bytes 3145728
  (5 shorter events, 0.1 us)
Async XLA Ops:
  8.0 11.5 %copy-start = (s32[1,8,5,16,512]{4,3,2,1,0:T(8,128)S(1)}, s32[1,8,5,16,512]{4,3,2,1,0:T(8,128)}, u32[]{:S(2)}) copy-start(s32[1,8,5,16,512]{4,3,2,1,0:T(8,128)} %param.7) | copy-start | bytes 3932164
  8.0 32.9 %all-gather.3.cloned.1.call-start = ((), (), s32[]{:S(2)}) async-start(), calls=%async_computation.2 | async-start | bytes 1179648 | tf_op jit(solution)/shard_map/all_gather | solution.py:77
  14.4 141.0 %all-reduce.7.cloned.1.call-start = ((), (), s32[]{:S(2)}) async-start(), calls=%async_computation.1 | async-start | bytes 3145728 | tf_op jit(solution)/shard_map/psum | solution.py:92
  19.3 181.5 %all-reduce.5.cloned.1.call-start = ((), (), s32[]{:S(2)}) async-start(), calls=%async_computation | async-start | bytes 1572864 | tf_op jit(solution)/shard_map/psum | solution.py:91
  40.9 10.5 %copy-start.2 = (bf16[1,8,128,512]{3,2,1,0:T(8,128)(2,1)S(1)}, bf16[1,8,128,512]{3,2,1,0:T(8,128)(2,1)}, u32[]{:S(2)}) copy-start(bf16[1,8,128,512]{3,2,1,0:T(8,128)(2,1)} %param.6) | copy-start | bytes 3145732
  40.9 10.5 %copy-start.3 = (bf16[2048,256]{1,0:T(8,128)(2,1)S(1)}, bf16[2048,256]{1,0:T(8,128)(2,1)}, u32[]{:S(2)}) copy-start(bf16[2048,256]{1,0:T(8,128)(2,1)} %all-gather.3.cloned.1.call-done) | copy-start | bytes 3145732
  51.3 11.0 %copy-start.1 = (bf16[1,1,128,256]{3,2,1,0:T(8,128)(2,1)S(1)}, bf16[1,1,128,256]{3,2,1,0:T(8,128)(2,1)}, u32[]{:S(2)}) copy-start(bf16[1,1,128,256]{3,2,1,0:T(8,128)(2,1)} %param.11) | copy-start | bytes 196612
Sparse Core Ops, SparseCore 0:
  14.5 26.3 all-gather.2
Sparse Core Ops, SparseCore 1:
  20.7 134.6 all-reduce.6
  158.2 42.5 all-reduce.4
where the time goes:
time: 214 us; the launch traced here: 213 us
  waiting for transfers between devices  109 us (51%)
  blocking collectives  39.3 us (18%)
  other arithmetic  16.6 us (8%)
  matrix products  16.1 us (8%)
  local copies, waits for them, and re-layouts  15.8 us (7%)
  between operations  15.6 us (7%)
    psum x1, waiting for transfers between devices, on_device(): lax.psum((weight_grad, bias_one, bias_two), ('feat', 'rep'))  53.7 us
    psum x1, waiting for transfers between devices, on_device(): grad_w1 = lax.psum(running, 'rep')  45.4 us
    psum x1, blocking collectives, on_device(): lax.psum((weight_grad, bias_one, bias_two), ('feat', 'rep'))  39.3 us
    reduce_sum x1, other arithmetic, unpack(): degree = jnp.sum(dense, axis=-1).astype(jnp.float32)  10.9 us
    shift_right_arithmetic x5, local copies, waits for them, and re-layouts, unpack(): jnp.right_shift(packed[..., None, :], shifts[:, None])  10.6 us
    all_gather x1, waiting for transfers between devices, on_device(): piece = lax.all_gather(hidden_grad[None], 'feat', axis=0, tiled=True)  10.1 us
    dot_general x1, matrix products, panel_terms(): jnp.einsum('brdc,bdh->rch', gathered, grad_block, preferred_element_type=...  9.46 us
    unnamed x10, local copies, waits for them, and re-layouts  4.85 us
  transfers between devices with their start and end apart: 3, of which 3 were waited for; matrix products, arithmetic and copies ran while one was open for 18% of the time, Pallas kernels for 0%

commit v1 on v0

--- a/solution.py
+++ b/solution.py
@@ -1,8 +1,22 @@
+import functools
 import math
 import jax
 import jax.numpy as jnp
 from jax import lax
 from jax.sharding import PartitionSpec as P
+
+
+def chunk_balance(block_in, comm_axis):
+    kept_arr = block_in
+    num_devices = lax.axis_size(comm_axis)
+    for s in [
+        [(at, at ^ d) for at in range(num_devices)] for d in (1, 2, 4, 8, 16) if d < num_devices
+    ]:
+        kept_arr = kept_arr + lax.ppermute(kept_arr, axis_name=comm_axis, perm=s)
+    return kept_arr
+
+
+bands_lay = functools.partial(chunk_balance, comm_axis="rep")
 
 
 def unpack(packed):
@@ -88,7 +102,7 @@
         return (running + panel_terms(inputs[0], inputs[1], inputs[2]), None)
 
     running, unused = lax.scan(one_turn, initial, (word_block, column_block, grad_block))
-    grad_w1 = lax.psum(running, "rep")
+    grad_w1 = bands_lay(running)
     grad_w2, grad_b1, grad_b2 = lax.psum((weight_grad, bias_one, bias_two), ("feat", "rep"))
     return (grad_w1, grad_b1, grad_w2, grad_b2)
 

time: 214 us -> 243 us (1.14)
  blocking collectives: 39.3 us -> 61.3 us
  starting transfers between devices: 0.31 us -> 4.03 us
  waiting for transfers between devices: 109 us -> 112 us
  other arithmetic: 16.6 us -> 19.3 us
    psum x1 -> x0, waiting for transfers between devices: 45.4 us -> none  [on_device(): grad_w1 = lax.psum(running, 'rep')]
    psum x1, waiting for transfers between devices: 53.7 us -> 80.4 us  [on_device(): lax.psum((weight_grad, bias_one, bias_two), ('feat', 'rep'))]
    psum x1, blocking collectives: 39.3 us -> 61.3 us  [on_device(): lax.psum((weight_grad, bias_one, bias_two), ('feat', 'rep'))]
    ppermute x0 -> x2, waiting for transfers between devices: none -> 17.6 us  [chunk_balance(): kept_arr = kept_arr + lax.ppermute(kept_arr, axis_name=comm_axis, perm=s)]
    ppermute x0 -> x2, starting transfers between devices: none -> 3.95 us  [chunk_balance(): kept_arr = kept_arr + lax.ppermute(kept_arr, axis_name=comm_axis, perm=s)]
    all_gather x1, waiting for transfers between devices: 10.1 us -> 13.7 us  [on_device(): piece = lax.all_gather(hidden_grad[None], 'feat', axis=0, tiled=True)]
  transfers between devices with their start and end apart: 3 -> 4, of which waited for: 3 -> 3; matrix products, arithmetic and copies ran while one was open for 18% -> 7% of each run, Pallas kernels for 0% -> 0%
where the time goes in v1:
time: 243 us
  waiting for transfers between devices  112 us (46%)
  blocking collectives  61.3 us (25%)
  other arithmetic  19.3 us (8%)
  matrix products  15.9 us (7%)
  between operations  15.6 us (6%)
  local copies, waits for them, and re-layouts  14.8 us (6%)
  starting transfers between devices  4.03 us (2%)
    psum x1, waiting for transfers between devices, on_device(): lax.psum((weight_grad, bias_one, bias_two), ('feat', 'rep'))  80.4 us
    psum x1, blocking collectives, on_device(): lax.psum((weight_grad, bias_one, bias_two), ('feat', 'rep'))  61.3 us
    ppermute x2, waiting for transfers between devices, chunk_balance(): kept_arr = kept_arr + lax.ppermute(kept_arr, axis_name=comm_axis, perm=s)  17.6 us
    all_gather x1, waiting for transfers between devices, on_device(): piece = lax.all_gather(hidden_grad[None], 'feat', axis=0, tiled=True)  13.7 us
    reduce_sum x1, other arithmetic, unpack(): degree = jnp.sum(dense, axis=-1).astype(jnp.float32)  12.2 us
    shift_right_arithmetic x5, local copies, waits for them, and re-layouts, unpack(): jnp.right_shift(packed[..., None, :], shifts[:, None])  11.7 us
    dot_general x1, matrix products, panel_terms(): jnp.einsum('brdc,bdh->rch', gathered, grad_block, preferred_element_type=...  9.39 us
  transfers between devices with their start and end apart: 4, of which 3 were waited for; matrix products, arithmetic and copies ran while one was open for 7% of the time, Pallas kernels for 0%

profile of v1, /device:TPU:0, one launch (start us, length us, event | category | flops | bytes accessed | tf_op | source)
XLA Modules:
  0.0 242.5 jit_solution(12300111847863722914)
XLA Ops:
  8.0 0.0 all-gather.3.cloned.1.call-start
  8.0 1.5 fusion.28
  9.6 0.1 div.22
  9.7 0.1 shift_right_arithmetic.72
  9.8 0.9 fusion.27
  10.7 1.1 fusion.37
  11.8 2.4 convert_reduce_fusion
  14.3 0.0 all-gather.3.cloned.1.call-update
  14.3 0.0 all-reduce.4.cloned.1.call-start
  14.3 12.2 %and_reduce_fusion = s32[8,5,16,16]{3,2,1,0:T(8,128)S(1)} fusion(s32[8,5,16,512]{3,2,1,0:T(8,128)} %bitcast.90), kind=kLoop, calls=%fused_computation.3 | loop fusion | flops 15718400 | bytes 1351680 | tf_op jit(solution)/shard_map/while/body/eval_jaxpr/reduce_sum | solution.py:26
  26.5 0.1 maximum_divide_fusion
  26.6 0.2 reshape.90
  26.8 0.1 shift_right_arithmetic.81
  26.9 13.7 %all-gather.3.cloned.1.call-done = bf16[2048,256]{1,0:T(8,128)(2,1)} async-done(((bf16[256,256]{1,0:T(8,128)(2,1)}), bf16[2048,256]{1,0:T(8,128)(2,1)}) %all-gather.3.cloned.1.call-update) | async-done | bytes 1048592 | tf_op jit(solution)/shard_map/all_gather | solution.py:91
  40.5 2.0 convolution_bitcast_fusion.2
  42.5 0.1 copy.30
  42.7 0.0 copy-start.2
  42.7 11.5 %shift_right_arithmetic.78 = s32[8,5,16,16,512]{4,3,2,1,0:T(8,128)} broadcast(s32[8,5,16,512]{3,2,1,0:T(8,128)} %bitcast.91), dimensions={0,1,2,4} | broadcast | bytes 22282240 | tf_op jit(solution)/shard_map/while/body/eval_jaxpr/shift_right_arithmetic | solution.py:24
  54.2 0.0 copy-done.2
  54.2 0.0 copy-start.1
  54.2 0.0 copy-start
  54.2 9.4 %fusion.13 = f32[5,128,256]{2,1,0:T(8,128)S(1)} fusion(bf16[8,256,256,1]{2,1,0,3:T(8,128)(2,1)} %bitcast.97, f32[8,5,256]{2,0,1:T(8,128)S(1)} %copy.37, s32[8,5,256,512]{3,2,1,0:T(8,128)} %bitcast.89, s32[256]{0:T(256)S(1)} %shift_right_arithmetic.81, bf16[1,8,128,512]{3,2,1,0:T(8,128)(2,1)S(1)} %copy-done.2), kind=kOutput, calls=%fused_computation.14 | convolution fusion | flops 2031616000 | bytes 23766016 | tf_op jit(solution)/shard_map/while/body/eval_jaxpr/brdc,bdh->rch/dot_general | solution.py:70
  63.6 1.0 pad_maximum_fusion.1
  64.6 1.5 collective-permute-start
  66.1 0.0 copy-done.1
  66.1 0.0 copy-done
  66.1 0.2 convolution_bitcast_fusion.1
  66.3 0.7 fusion.19
  67.0 17.6 %collective-permute-done = f32[6,128,256]{2,1,0:T(8,128)} collective-permute-done((f32[6,128,256]{2,1,0:T(8,128)}, f32[6,128,256]{2,1,0:T(8,128)}, u32[]{:S(2)}, u32[]{:S(2)}) %collective-permute-start) | collective-permute-done | bytes 786464 | tf_op jit(solution)/shard_map/ppermute | solution.py:15
  84.6 1.3 fusion.59
  85.8 2.5 %collective-permute-start.1 = (f32[6,128,256]{2,1,0:T(8,128)S(1)}, f32[6,128,256]{2,1,0:T(8,128)S(1)}, u32[]{:S(2)}, u32[]{:S(2)}) collective-permute-start(f32[6,128,256]{2,1,0:T(8,128)S(1)} %fusion.59), channel_id=1, source_target_pairs={{0,2},{1,3},{2,0},{3,1},{4,6},{5,7},{6,4},{7,5},{8,10},{9,11},{10,... | collective-permute-start | bytes 2359304 | tf_op jit(solution)/shard_map/ppermute | solution.py:15
  88.3 1.3 pad_maximum_fusion
  89.6 0.0 all-reduce.4.cloned.1.call-update
  89.7 61.3 %all-reduce.1 = (f32[256]{0:T(256)}, f32[256]{0:T(256)}) all-reduce(f32[256]{0:T(256)S(1)} %get-tuple-element.23, f32[256]{0:T(256)S(1)} %fusion.40), channel_id=1, replica_groups=mesh['feat'=8,'rep'=4] {'feat','rep'}, use_global_device_ids=true, to_apply=%region_3.4 | all-reduce | flops 512 | bytes 4096 | tf_op jit(solution)/shard_map/psum | solution.py:106
  151.0 0.0 collective-permute-done.1
  151.0 1.0 add.23
  152.0 80.4 %all-reduce.4.cloned.1.call-done = f32[6,256,256]{2,1,0:T(8,128)} async-done(((f32[6,256,256]{2,1,0:T(8,128)}), f32[6,256,256]{2,1,0:T(8,128)}) %all-reduce.4.cloned.1.call-update) | async-done | bytes 1572880 | tf_op jit(solution)/shard_map/psum | solution.py:106
  232.3 2.7 %copy.51 = f32[6,256,256]{2,1,0:T(8,128)} copy(f32[6,256,256]{2,1,0:T(8,128)} %all-reduce.4.cloned.1.call-done) | data formatting | bytes 3145728
  (6 shorter events, 0.1 us)
Async XLA Ops:
  8.0 32.5 %all-gather.3.cloned.1.call-start = ((), (), s32[]{:S(2)}) async-start(), calls=%async_computation.1 | async-start | bytes 1179648 | tf_op jit(solution)/shard_map/all_gather | solution.py:91
  14.3 218.1 %all-reduce.4.cloned.1.call-start = ((), (), s32[]{:S(2)}) async-start(), calls=%async_computation | async-start | bytes 3145728 | tf_op jit(solution)/shard_map/psum | solution.py:106
  42.7 11.5 %copy-start.2 = (bf16[1,8,128,512]{3,2,1,0:T(8,128)(2,1)S(1)}, bf16[1,8,128,512]{3,2,1,0:T(8,128)(2,1)}, u32[]{:S(2)}) copy-start(bf16[1,8,128,512]{3,2,1,0:T(8,128)(2,1)} %param.6) | copy-start | bytes 3145732
  54.2 11.9 %copy-start.1 = (bf16[1,1,256,256]{3,2,1,0:T(8,128)(2,1)S(1)}, bf16[1,1,256,256]{3,2,1,0:T(8,128)(2,1)}, u32[]{:S(2)}) copy-start(bf16[1,1,256,256]{3,2,1,0:T(8,128)(2,1)} %param.8) | copy-start | bytes 393220
  54.2 11.9 %copy-start = (bf16[1,1,128,256]{3,2,1,0:T(8,128)(2,1)S(1)}, bf16[1,1,128,256]{3,2,1,0:T(8,128)(2,1)}, u32[]{:S(2)}) copy-start(bf16[1,1,128,256]{3,2,1,0:T(8,128)(2,1)} %param.11) | copy-start | bytes 196612
  64.6 20.0 %collective-permute-start = (f32[6,128,256]{2,1,0:T(8,128)}, f32[6,128,256]{2,1,0:T(8,128)}, u32[]{:S(2)}, u32[]{:S(2)}) collective-permute-start(f32[6,128,256]{2,1,0:T(8,128)} %pad_maximum_fusion.1), channel_id=1, source_target_pairs={{0,1},{1,0},{2,3},{3,2},{4,5},{5,4},{6,7},{7,6},{8,9},{9,8},{10,11... | collective-permute-start | bytes 2359304 | tf_op jit(solution)/shard_map/ppermute | solution.py:15
  85.8 65.1 %collective-permute-start.1 = (f32[6,128,256]{2,1,0:T(8,128)S(1)}, f32[6,128,256]{2,1,0:T(8,128)S(1)}, u32[]{:S(2)}, u32[]{:S(2)}) collective-permute-start(f32[6,128,256]{2,1,0:T(8,128)S(1)} %fusion.59), channel_id=1, source_target_pairs={{0,2},{1,3},{2,0},{3,1},{4,6},{5,7},{6,4},{7,5},{8,10},{9,11},{10,... | collective-permute-start | bytes 2359304 | tf_op jit(solution)/shard_map/ppermute | solution.py:15
Sparse Core Ops, SparseCore 0:
  14.4 26.0 all-gather.2
Sparse Core Ops, SparseCore 1:
  89.7 142.5 all-reduce.3
